TPU v7x, 32 devices: a whole 2x2x4 slice. The times are simulated.
32 devices in a mesh: uly: 2 (over y), blk: 16 (over z, x, core).
Axes of the slice: x: 2, y: 2, z: 4, core: 2. Of those that a mesh axis runs over, the one named last changes fastest.
Arguments:
- query_inputs: bfloat16 [4096, 2048], P(('blk', 'uly')), may hold values from -6 to 6
- key_inputs: bfloat16 [4096, 1024], P(('blk', 'uly')), may hold values from -6 to 6
- value_inputs: bfloat16 [4096, 1024], P(('blk', 'uly')), may hold values from -6 to 6
- forward_out: bfloat16 [4096, 2048], P(('blk', 'uly')), may hold values from -6 to 6
- output_gradient: bfloat16 [4096, 2048], P(('blk', 'uly')), may hold values from -4 to 4
- lse_parts: float32 [4096, 16, 2], P(('blk', 'uly')), may hold values from 3 to 247
- segment_ids: int32 [4096], P(('blk', 'uly')), may hold values from 0 to 31, never falling along the last dimension, each value on 1 to 512 neighbouring positions
Outputs:
- query_grad: bfloat16 [4096, 2048], P(('blk', 'uly'))
- key_grad: bfloat16 [4096, 1024], P(('blk', 'uly'))
- value_grad: bfloat16 [4096, 1024], P(('blk', 'uly'))
Inputs may be any that keep to these rules, and one draw needn't show every extreme that they name: `segment_ids`: never falls along the sequence; every document holds 1 to 512 tokens, and some document exactly 512.
All inputs are finite; a program needn't handle non-finite values.
Results may differ from a plain program's by a relative error of at most 0.0051.
Values may be sent and summed in bfloat16 or wider, within the bound.
A program may use at most 128 MiB of HBM per device.

v0:
```python
import math

import jax
import jax.numpy as jnp
from jax import lax
from jax.sharding import PartitionSpec as P

HEAD_SIZE = 128
QUERY_HEADS = 16
KEY_VALUE_HEADS = 8
HOPS = 2
QBLOCK = 512


def from_behind(block, axis, distance):
    devices = range(lax.axis_size(axis))
    route = [(i - distance, i) for i in devices if i - distance in devices]
    return lax.ppermute(block, axis, route)


def merge_parts(partials):
    highest = jnp.max(partials, axis=-1)
    return highest + jnp.log(jnp.sum(jnp.exp(partials - highest[..., None]), axis=-1))


def row_delta(grad_rows, out_rows):
    row_total = grad_rows.shape[0]
    products = grad_rows.astype(jnp.float32) * out_rows.astype(jnp.float32)
    return jnp.sum(products.reshape(row_total, -1, HEAD_SIZE), axis=-1)


def tile_grads(query_blk, grad_blk, lse_blk, delta_blk, key_blk, value_blk, allowed):
    score_scale = 1.0 / math.sqrt(HEAD_SIZE)
    scores = (
        jnp.einsum("mhgd,nhd->hgmn", query_blk, key_blk, preferred_element_type=jnp.float32)
        * score_scale
    )
    weights = jnp.where(allowed, jnp.exp(scores - lse_blk), 0.0)
    value_portion = jnp.einsum(
        "hgmn,mhgd->nhd", weights.astype(jnp.bfloat16), grad_blk, preferred_element_type=jnp.float32
    )
    prob_grad = jnp.einsum(
        "mhgd,nhd->hgmn", grad_blk, value_blk, preferred_element_type=jnp.float32
    )
    score_grad = (weights * (prob_grad - delta_blk)).astype(jnp.bfloat16)
    query_part = (
        jnp.einsum("hgmn,nhd->mhgd", score_grad, key_blk, preferred_element_type=jnp.float32)
        * score_scale
    )
    key_portion = (
        jnp.einsum("hgmn,mhgd->nhd", score_grad, query_blk, preferred_element_type=jnp.float32)
        * score_scale
    )
    return (query_part, key_portion, value_portion)


def per_device(
    query_inputs, key_inputs, value_inputs, forward_out, output_gradient, lse_parts, segment_ids
):
    uly_count = lax.axis_size("uly")
    blk_place = lax.axis_index("blk")
    tok_local = query_inputs.shape[0]
    row_count = tok_local * uly_count
    group_width = QUERY_HEADS // KEY_VALUE_HEADS
    query_loc, grad_loc, key_loc, value_loc, out_loc = (
        lax.all_to_all(query_inputs, "uly", split_axis=1, concat_axis=0, tiled=True),
        lax.all_to_all(output_gradient, "uly", split_axis=1, concat_axis=0, tiled=True),
        lax.all_to_all(key_inputs, "uly", split_axis=1, concat_axis=0, tiled=True),
        lax.all_to_all(value_inputs, "uly", split_axis=1, concat_axis=0, tiled=True),
        lax.all_to_all(forward_out, "uly", split_axis=1, concat_axis=0, tiled=True),
    )
    parts_loc = lax.all_to_all(
        lse_parts.reshape(tok_local, -1), "uly", split_axis=1, concat_axis=0, tiled=True
    )
    lse_loc = merge_parts(parts_loc.reshape(row_count, -1, 2))
    delta_loc = row_delta(grad_loc, out_loc)
    ids_loc = lax.all_gather(segment_ids, "uly", axis=0, tiled=True)
    kv_heads = key_loc.shape[1] // HEAD_SIZE
    query_quad = query_loc.reshape(row_count, kv_heads, group_width, HEAD_SIZE)
    gradient_quad = grad_loc.reshape(row_count, kv_heads, group_width, HEAD_SIZE)
    logsumexp_cube = lse_loc.reshape(row_count, kv_heads, group_width).transpose(1, 2, 0)[..., None]
    delta_cube = delta_loc.reshape(row_count, kv_heads, group_width).transpose(1, 2, 0)[..., None]
    key_cube = key_loc.reshape(row_count, kv_heads, HEAD_SIZE)
    value_cube = value_loc.reshape(row_count, kv_heads, HEAD_SIZE)
    rows_per_block = min(QBLOCK, row_count)
    block_total = row_count // rows_per_block
    position = jnp.arange(row_count, dtype=jnp.int32)
    query_parts = []
    key_gradient_running = jnp.zeros((row_count, kv_heads, HEAD_SIZE), jnp.float32)
    value_gradient_running = jnp.zeros((row_count, kv_heads, HEAD_SIZE), jnp.float32)
    for block_index in range(block_total):
        leading_row = block_index * rows_per_block
        finish = leading_row + rows_per_block
        allowed = (position[None, :finish] <= position[leading_row:finish, None]) & (
            ids_loc[None, :finish] == ids_loc[leading_row:finish, None]
        )
        tile_out = tile_grads(
            query_quad[leading_row:finish],
            gradient_quad[leading_row:finish],
            logsumexp_cube[:, :, leading_row:finish],
            delta_cube[:, :, leading_row:finish],
            key_cube[:finish],
            value_cube[:finish],
            allowed,
        )
        query_parts.append(tile_out[0])
        padding = ((0, row_count - finish), (0, 0), (0, 0))
        key_gradient_running = key_gradient_running + jnp.pad(tile_out[1], padding)
        value_gradient_running = value_gradient_running + jnp.pad(tile_out[2], padding)
    query_acc = jnp.concatenate(query_parts, axis=0)
    stacked_kv = jnp.stack([key_loc, value_loc])
    moved_kv = stacked_kv
    moved_ids = ids_loc
    key_parts = []
    for hop_index in range(1, HOPS + 1):
        moved_kv = from_behind(stacked_kv, "blk", hop_index)
        moved_ids = from_behind(ids_loc, "blk", hop_index)
        live = (blk_place >= hop_index) & (moved_ids[-1] == ids_loc[0])
        moved_key = moved_kv[0].reshape(row_count, kv_heads, HEAD_SIZE)
        moved_value = moved_kv[1].reshape(row_count, kv_heads, HEAD_SIZE)

        def compute_tile(unused):
            query_pieces = []
            key_sum = jnp.zeros((row_count, kv_heads, HEAD_SIZE), jnp.float32)
            value_sum = jnp.zeros((row_count, kv_heads, HEAD_SIZE), jnp.float32)
            for block_index in range(block_total):
                leading_row = block_index * rows_per_block
                finish = leading_row + rows_per_block
                allowed = moved_ids[None, :] == ids_loc[leading_row:finish, None]
                tile_out = tile_grads(
                    query_quad[leading_row:finish],
                    gradient_quad[leading_row:finish],
                    logsumexp_cube[:, :, leading_row:finish],
                    delta_cube[:, :, leading_row:finish],
                    moved_key,
                    moved_value,
                    allowed,
                )
                query_pieces.append(tile_out[0])
                key_sum = key_sum + tile_out[1]
                value_sum = value_sum + tile_out[2]
            stacked = jnp.stack([key_sum.reshape(row_count, -1), value_sum.reshape(row_count, -1)])
            return (jnp.concatenate(query_pieces, axis=0), stacked)

        def skip_tile(unused):
            return (
                jnp.zeros((row_count, kv_heads, group_width, HEAD_SIZE), jnp.float32),
                jnp.zeros((2, row_count, kv_heads * HEAD_SIZE), jnp.float32),
            )

        query_more, key_more = lax.cond(live, compute_tile, skip_tile, 0)
        query_acc = query_acc + query_more
        key_parts.append(key_more)
    returned = jnp.zeros((2, row_count, kv_heads * HEAD_SIZE), jnp.float32)
    for hop_index in range(1, HOPS + 1):
        returned = returned + from_behind(key_parts[hop_index - 1], "blk", -hop_index)
    key_total = (key_gradient_running.reshape(row_count, -1) + returned[0]).astype(jnp.bfloat16)
    value_total = (value_gradient_running.reshape(row_count, -1) + returned[1]).astype(jnp.bfloat16)
    query_total = query_acc.reshape(row_count, -1).astype(jnp.bfloat16)
    query_grad, key_grad, value_grad = (
        lax.all_to_all(query_total, "uly", split_axis=0, concat_axis=1, tiled=True),
        lax.all_to_all(key_total, "uly", split_axis=0, concat_axis=1, tiled=True),
        lax.all_to_all(value_total, "uly", split_axis=0, concat_axis=1, tiled=True),
    )
    return (query_grad, key_grad, value_grad)


def solution(mesh):
    placed = (
        P(("blk", "uly"), None),
        P(("blk", "uly"), None),
        P(("blk", "uly"), None),
        P(("blk", "uly"), None),
        P(("blk", "uly"), None),
        P(("blk", "uly"), None, None),
        P(("blk", "uly")),
    )
    return jax.shard_map(
        per_device,
        mesh=mesh,
        in_specs=placed,
        out_specs=(P(("blk", "uly"), None), P(("blk", "uly"), None), P(("blk", "uly"), None)),
        check_vma=False,
    )
```

profile of v0, /device:TPU:0, one launch (start us, length us, event | category | flops | bytes accessed | tf_op | source)
XLA Modules:
  0.0 147.4 jit_solution(7984379366214825627)
XLA Ops:
  0.7 4.4 %all-to-all-start.2 = ((f32[128,2,16]{0,2,1:T(8,128)}), f32[128,2,16]{0,2,1:T(8,128)S(1)}, u32[]{:S(2)}, u32[]{:S(2)}) async-start(f32[128,2,16]{0,2,1:T(8,128)} %bitcast.239), calls=%async_computation.2 | async-start | bytes 32768 | tf_op jit(solution)/shard_map/all_to_all | solution.py:72
  6.8 2.1 %all-to-all-done.2 = f32[128,2,16]{0,2,1:T(8,128)S(1)} async-done(((f32[128,2,16]{0,2,1:T(8,128)}), f32[128,2,16]{0,2,1:T(8,128)S(1)}, u32[]{:S(2)}, u32[]{:S(2)}) %all-to-all-start.2) | async-done | bytes 16416 | tf_op jit(solution)/shard_map/all_to_all | solution.py:72
  8.9 3.4 %all-to-all-start = ((bf16[128,2,512]{2,0,1:T(8,128)(2,1)}), bf16[128,2,512]{2,0,1:T(8,128)(2,1)S(1)}, u32[]{:S(2)}, u32[]{:S(2)}) async-start(bf16[128,2,512]{2,0,1:T(8,128)(2,1)} %bitcast.192), calls=%async_computation | async-start | bytes 524288 | tf_op jit(solution)/shard_map/all_to_all | solution.py:68
  12.4 1.7 %copy.288 = bf16[16,2,8,512]{3,2,0,1:T(8,128)(2,1)} copy(bf16[16,2,8,512]{3,2,1,0:T(8,128)(2,1)} %bitcast.226) | data formatting | bytes 524288 | tf_op jit(solution)/shard_map/all_to_all | solution.py:69
  14.1 3.4 %all-to-all-done = bf16[128,2,512]{2,0,1:T(8,128)(2,1)S(1)} async-done(((bf16[128,2,512]{2,0,1:T(8,128)(2,1)}), bf16[128,2,512]{2,0,1:T(8,128)(2,1)S(1)}, u32[]{:S(2)}, u32[]{:S(2)}) %all-to-all-start) | async-done | bytes 262176 | tf_op jit(solution)/shard_map/all_to_all | solution.py:68
  17.5 3.4 %all-to-all-start.3 = ((bf16[128,2,512]{2,0,1:T(8,128)(2,1)}), bf16[128,2,512]{2,0,1:T(8,128)(2,1)S(1)}, u32[]{:S(2)}, u32[]{:S(2)}) async-start(bf16[128,2,512]{2,0,1:T(8,128)(2,1)} %bitcast.191), calls=%async_computation.3 | async-start | bytes 524288 | tf_op jit(solution)/shard_map/all_to_all | solution.py:69
  21.0 5.2 %all-gather = s32[2,1,128]{2,1,0:T(1,128)S(1)} all-gather(s32[1,1,128]{2,1,0:T(1,128)S(1)} %bitcast.245), channel_id=1, replica_groups=mesh['uly'=2,'blk'=16] {'uly'}, dimensions={0}, use_global_device_ids=true | all-gather | bytes 1536 | tf_op jit(solution)/shard_map/all_gather | solution.py:77
  27.5 4.5 %collective-permute-start.2 = (s32[256]{0:T(256)S(1)}, s32[256]{0:T(256)S(1)}, u32[]{:S(2)}, u32[]{:S(2)}) collective-permute-start(s32[256]{0:T(256)S(1)} %bitcast.234), channel_id=1, source_target_pairs={{0,2},{1,3},{2,4},{3,5},{4,6},{5,7},{6,8},{7,9},{8,10},{9,11},{10,... | collective-permute-start | bytes 3080 | tf_op jit(solution)/shard_map/ppermute | solution.py:18
  32.8 3.5 %all-to-all-start.4 = ((bf16[128,2,1024]{2,0,1:T(8,128)(2,1)}), bf16[128,2,1024]{2,0,1:T(8,128)(2,1)S(1)}, u32[]{:S(2)}, u32[]{:S(2)}) async-start(bf16[128,2,1024]{2,0,1:T(8,128)(2,1)} %bitcast.189), calls=%async_computation.4 | async-start | bytes 1048576 | tf_op jit(solution)/shard_map/all_to_all | solution.py:67
  42.6 2.7 %all-to-all-done.4 = bf16[128,2,1024]{2,0,1:T(8,128)(2,1)S(1)} async-done(((bf16[128,2,1024]{2,0,1:T(8,128)(2,1)}), bf16[128,2,1024]{2,0,1:T(8,128)(2,1)S(1)}, u32[]{:S(2)}, u32[]{:S(2)}) %all-to-all-start.4) | async-done | bytes 524320 | tf_op jit(solution)/shard_map/all_to_all | solution.py:67
  45.3 3.5 %all-to-all-start.5 = ((bf16[128,2,1024]{2,0,1:T(8,128)(2,1)}), bf16[128,2,1024]{2,0,1:T(8,128)(2,1)S(1)}, u32[]{:S(2)}, u32[]{:S(2)}) async-start(bf16[128,2,1024]{2,0,1:T(8,128)(2,1)} %bitcast.188), calls=%async_computation.5 | async-start | bytes 1048576 | tf_op jit(solution)/shard_map/all_to_all | solution.py:70
  49.9 2.9 %collective-permute-start.1 = (bf16[2,256,512]{1,2,0:T(8,128)(2,1)}, bf16[2,256,512]{1,2,0:T(8,128)(2,1)}, u32[]{:S(2)}, u32[]{:S(2)}) collective-permute-start(bf16[2,256,512]{1,2,0:T(8,128)(2,1)} %pad_maximum_fusion.2), channel_id=1, source_target_pairs={{0,1},{1,2},{2,3},{3,4},{4,5},{5,6},{6,7},{7,8},{8,9},{9,10},{10,1... | collective-permute-start | bytes 1572872 | tf_op jit(solution)/shard_map/ppermute | solution.py:18
  52.9 3.5 %collective-permute-start.3 = (bf16[2,256,512]{1,2,0:T(8,128)(2,1)}, bf16[2,256,512]{1,2,0:T(8,128)(2,1)}, u32[]{:S(2)}, u32[]{:S(2)}) collective-permute-start(bf16[2,256,512]{1,2,0:T(8,128)(2,1)} %pad_maximum_fusion.2), channel_id=1, source_target_pairs={{0,2},{1,3},{2,4},{3,5},{4,6},{5,7},{6,8},{7,9},{8,10},{9,11},{10,... | collective-permute-start | bytes 1572872 | tf_op jit(solution)/shard_map/ppermute | solution.py:18
  57.6 3.5 %all-to-all-start.1 = ((bf16[128,2,1024]{2,0,1:T(8,128)(2,1)}), bf16[128,2,1024]{2,0,1:T(8,128)(2,1)S(1)}, u32[]{:S(2)}, u32[]{:S(2)}) async-start(bf16[128,2,1024]{2,0,1:T(8,128)(2,1)} %bitcast.190), calls=%async_computation.1 | async-start | bytes 1048576 | tf_op jit(solution)/shard_map/all_to_all | solution.py:66
  61.9 8.2 %all-to-all-done.1 = bf16[128,2,1024]{2,0,1:T(8,128)(2,1)S(1)} async-done(((bf16[128,2,1024]{2,0,1:T(8,128)(2,1)}), bf16[128,2,1024]{2,0,1:T(8,128)(2,1)S(1)}, u32[]{:S(2)}, u32[]{:S(2)}) %all-to-all-start.1) | async-done | bytes 524320 | tf_op jit(solution)/shard_map/all_to_all | solution.py:66
  72.9 2.2 %conditional.2 = (f32[256,4,2,128]{3,0,2,1:T(8,128)}, f32[2,256,512]{1,2,0:T(8,128)}) conditional(s32[]{:T(128)} %convert_element_type.56, () %tuple.24, (s32[256]{0:T(256)S(1)}, s32[256]{0:T(256)S(1)}, bf16[2,256,512]{1,2,0:T(8,128)(2,1)}, bf16[256,4,2,128]{3,2,1,0:T(2,128)(2,1)S(1)}, f32[4,2,256,1]{2,1,0,3:T(2,128)S(1)}, ...), branch_computations={%region_3.4_spmd, %region_4.5_spmd} | conditional | flops 675479552 | bytes 33441920 | solution.py:151
  76.3 2.1 %conditional.3 = (f32[256,4,2,128]{3,0,2,1:T(8,128)}, f32[2,256,512]{1,2,0:T(8,128)}) conditional(s32[]{:T(128)} %convert_element_type.57, () %tuple.26, (s32[256]{0:T(256)S(1)}, s32[256]{0:T(256)S(1)}, bf16[2,256,512]{1,2,0:T(8,128)(2,1)}, bf16[256,4,2,128]{3,2,1,0:T(2,128)(2,1)S(1)}, f32[4,2,256,1]{2,1,0,3:T(2,128)S(1)}, ...), branch_computations={%region_5.6_spmd, %region_6.7_spmd} | conditional | flops 675479552 | bytes 33441920 | solution.py:151
  86.1 1.7 %add_convert_fusion = bf16[256,4,2,128]{3,0,2,1:T(8,128)(2,1)S(1)} fusion(f32[256,4,2,128]{3,0,2,1:T(8,128)} %get-tuple-element.60, f32[256,4,2,128]{3,0,2,1:T(8,128)S(1)} %fusion.20, f32[256,4,2,128]{3,0,2,1:T(8,128)} %get-tuple-element.59), kind=kLoop, calls=%fused_computation.42 | loop fusion | flops 786432 | bytes 3670016 | tf_op jit(solution)/shard_map/convert_element_type | solution.py:159
  89.6 3.5 %all-to-all-start.6 = ((bf16[2,128,1024]{2,1,0:T(8,128)(2,1)}), bf16[2,128,1024]{2,1,0:T(8,128)(2,1)S(1)}, u32[]{:S(2)}, u32[]{:S(2)}) async-start(bf16[2,128,1024]{2,1,0:T(8,128)(2,1)} %convert_element_type.59), calls=%async_computation.6 | async-start | bytes 1048576 | tf_op jit(solution)/shard_map/all_to_all | solution.py:161
  93.1 32.8 %collective-permute-done.5 = f32[2,256,512]{1,2,0:T(8,128)} collective-permute-done((f32[2,256,512]{1,2,0:T(8,128)}, f32[2,256,512]{1,2,0:T(8,128)}, u32[]{:S(2)}, u32[]{:S(2)}) %collective-permute-start.5) | collective-permute-done | bytes 1048608 | tf_op jit(solution)/shard_map/ppermute | solution.py:18
  128.8 3.4 %all-to-all-start.7 = ((bf16[2,128,512]{2,1,0:T(8,128)(2,1)}), bf16[2,128,512]{2,1,0:T(8,128)(2,1)S(1)}, u32[]{:S(2)}, u32[]{:S(2)}) async-start(bf16[2,128,512]{2,1,0:T(8,128)(2,1)} %add_convert_fusion.2), calls=%async_computation.7 | async-start | bytes 524288 | tf_op jit(solution)/shard_map/all_to_all | solution.py:162
  133.0 4.7 %all-to-all-done.7 = bf16[2,128,512]{2,1,0:T(8,128)(2,1)S(1)} async-done(((bf16[2,128,512]{2,1,0:T(8,128)(2,1)}), bf16[2,128,512]{2,1,0:T(8,128)(2,1)S(1)}, u32[]{:S(2)}, u32[]{:S(2)}) %all-to-all-start.7) | async-done | bytes 262176 | tf_op jit(solution)/shard_map/all_to_all | solution.py:162
  137.7 3.4 %all-to-all-start.8 = ((bf16[2,128,512]{2,1,0:T(8,128)(2,1)}), bf16[2,128,512]{2,1,0:T(8,128)(2,1)S(1)}, u32[]{:S(2)}, u32[]{:S(2)}) async-start(bf16[2,128,512]{2,1,0:T(8,128)(2,1)} %add_convert_fusion.1), calls=%async_computation.8 | async-start | bytes 524288 | tf_op jit(solution)/shard_map/all_to_all | solution.py:163
  143.5 2.8 %all-to-all-done.8 = bf16[2,128,512]{2,1,0:T(8,128)(2,1)S(1)} async-done(((bf16[2,128,512]{2,1,0:T(8,128)(2,1)}), bf16[2,128,512]{2,1,0:T(8,128)(2,1)S(1)}, u32[]{:S(2)}, u32[]{:S(2)}) %all-to-all-start.8) | async-done | bytes 262176 | tf_op jit(solution)/shard_map/all_to_all | solution.py:163
  (76 shorter events, 35.2 us)
Async XLA Ops:
  0.6 20.4 %copy-start.13 = (s32[128]{0:T(128)S(1)}, s32[128]{0:T(128)}, u32[]{:S(2)}) copy-start(s32[128]{0:T(128)} %param.17) | copy-start | bytes 1540
  0.6 31.4 %copy-start.10 = (bf16[128,2048]{1,0:T(8,128)(2,1)S(1)}, bf16[128,2048]{1,0:T(8,128)(2,1)}, u32[]{:S(2)}) copy-start(bf16[128,2048]{1,0:T(8,128)(2,1)} %param.15) | copy-start | bytes 1572868
  0.7 8.3 %all-to-all-start.2 = ((f32[128,2,16]{0,2,1:T(8,128)}), f32[128,2,16]{0,2,1:T(8,128)S(1)}, u32[]{:S(2)}, u32[]{:S(2)}) async-start(f32[128,2,16]{0,2,1:T(8,128)} %bitcast.239), calls=%async_computation.2 | async-start | bytes 32768 | tf_op jit(solution)/shard_map/all_to_all | solution.py:72
  5.1 31.9 %copy-start.11 = (bf16[128,2048]{1,0:T(8,128)(2,1)S(1)}, bf16[128,2048]{1,0:T(8,128)(2,1)}, u32[]{:S(2)}) copy-start(bf16[128,2048]{1,0:T(8,128)(2,1)} %param.14) | copy-start | bytes 1572868
  8.9 8.6 %all-to-all-start = ((bf16[128,2,512]{2,0,1:T(8,128)(2,1)}), bf16[128,2,512]{2,0,1:T(8,128)(2,1)S(1)}, u32[]{:S(2)}, u32[]{:S(2)}) async-start(bf16[128,2,512]{2,0,1:T(8,128)(2,1)} %bitcast.192), calls=%async_computation | async-start | bytes 524288 | tf_op jit(solution)/shard_map/all_to_all | solution.py:68
  12.4 25.4 %copy-start.12 = (bf16[128,2048]{1,0:T(8,128)(2,1)S(1)}, bf16[128,2048]{1,0:T(8,128)(2,1)}, u32[]{:S(2)}) copy-start(bf16[128,2048]{1,0:T(8,128)(2,1)} %param.11) | copy-start | bytes 1572868
  17.5 15.3 %all-to-all-start.3 = ((bf16[128,2,512]{2,0,1:T(8,128)(2,1)}), bf16[128,2,512]{2,0,1:T(8,128)(2,1)S(1)}, u32[]{:S(2)}, u32[]{:S(2)}) async-start(bf16[128,2,512]{2,0,1:T(8,128)(2,1)} %bitcast.191), calls=%async_computation.3 | async-start | bytes 524288 | tf_op jit(solution)/shard_map/all_to_all | solution.py:69
  26.2 12.4 %collective-permute-start = (s32[256]{0:T(256)S(1)}, s32[256]{0:T(256)S(1)}, u32[]{:S(2)}, u32[]{:S(2)}) collective-permute-start(s32[256]{0:T(256)S(1)} %bitcast.233), channel_id=1, source_target_pairs={{0,1},{1,2},{2,3},{3,4},{4,5},{5,6},{6,7},{7,8},{8,9},{9,10},{10,1... | collective-permute-start | bytes 3080 | tf_op jit(solution)/shard_map/ppermute | solution.py:18
  27.5 13.0 %collective-permute-start.2 = (s32[256]{0:T(256)S(1)}, s32[256]{0:T(256)S(1)}, u32[]{:S(2)}, u32[]{:S(2)}) collective-permute-start(s32[256]{0:T(256)S(1)} %bitcast.234), channel_id=1, source_target_pairs={{0,2},{1,3},{2,4},{3,5},{4,6},{5,7},{6,8},{7,9},{8,10},{9,11},{10,... | collective-permute-start | bytes 3080 | tf_op jit(solution)/shard_map/ppermute | solution.py:18
  32.8 12.5 %all-to-all-start.4 = ((bf16[128,2,1024]{2,0,1:T(8,128)(2,1)}), bf16[128,2,1024]{2,0,1:T(8,128)(2,1)S(1)}, u32[]{:S(2)}, u32[]{:S(2)}) async-start(bf16[128,2,1024]{2,0,1:T(8,128)(2,1)} %bitcast.189), calls=%async_computation.4 | async-start | bytes 1048576 | tf_op jit(solution)/shard_map/all_to_all | solution.py:67
  45.3 12.3 %all-to-all-start.5 = ((bf16[128,2,1024]{2,0,1:T(8,128)(2,1)}), bf16[128,2,1024]{2,0,1:T(8,128)(2,1)S(1)}, u32[]{:S(2)}, u32[]{:S(2)}) async-start(bf16[128,2,1024]{2,0,1:T(8,128)(2,1)} %bitcast.188), calls=%async_computation.5 | async-start | bytes 1048576 | tf_op jit(solution)/shard_map/all_to_all | solution.py:70
  49.9 22.9 %collective-permute-start.1 = (bf16[2,256,512]{1,2,0:T(8,128)(2,1)}, bf16[2,256,512]{1,2,0:T(8,128)(2,1)}, u32[]{:S(2)}, u32[]{:S(2)}) collective-permute-start(bf16[2,256,512]{1,2,0:T(8,128)(2,1)} %pad_maximum_fusion.2), channel_id=1, source_target_pairs={{0,1},{1,2},{2,3},{3,4},{4,5},{5,6},{6,7},{7,8},{8,9},{9,10},{10,1... | collective-permute-start | bytes 1572872 | tf_op jit(solution)/shard_map/ppermute | solution.py:18
  52.9 23.5 %collective-permute-start.3 = (bf16[2,256,512]{1,2,0:T(8,128)(2,1)}, bf16[2,256,512]{1,2,0:T(8,128)(2,1)}, u32[]{:S(2)}, u32[]{:S(2)}) collective-permute-start(bf16[2,256,512]{1,2,0:T(8,128)(2,1)} %pad_maximum_fusion.2), channel_id=1, source_target_pairs={{0,2},{1,3},{2,4},{3,5},{4,6},{5,7},{6,8},{7,9},{8,10},{9,11},{10,... | collective-permute-start | bytes 1572872 | tf_op jit(solution)/shard_map/ppermute | solution.py:18
  57.6 12.5 %all-to-all-start.1 = ((bf16[128,2,1024]{2,0,1:T(8,128)(2,1)}), bf16[128,2,1024]{2,0,1:T(8,128)(2,1)S(1)}, u32[]{:S(2)}, u32[]{:S(2)}) async-start(bf16[128,2,1024]{2,0,1:T(8,128)(2,1)} %bitcast.190), calls=%async_computation.1 | async-start | bytes 1048576 | tf_op jit(solution)/shard_map/all_to_all | solution.py:66
  70.5 1.0 copy-start.9
  75.0 18.0 %collective-permute-start.4 = (f32[2,256,512]{1,2,0:T(8,128)}, f32[2,256,512]{1,2,0:T(8,128)}, u32[]{:S(2)}, u32[]{:S(2)}) collective-permute-start(f32[2,256,512]{1,2,0:T(8,128)} %get-tuple-element.61), channel_id=1, source_target_pairs={{1,0},{2,1},{3,2},{4,3},{5,4},{6,5},{7,6},{8,7},{9,8},{10,9},{11,1... | collective-permute-start | bytes 3145736 | tf_op jit(solution)/shard_map/ppermute | solution.py:18
  78.4 47.4 %collective-permute-start.5 = (f32[2,256,512]{1,2,0:T(8,128)}, f32[2,256,512]{1,2,0:T(8,128)}, u32[]{:S(2)}, u32[]{:S(2)}) collective-permute-start(f32[2,256,512]{1,2,0:T(8,128)} %get-tuple-element.62), channel_id=1, source_target_pairs={{2,0},{3,1},{4,2},{5,3},{6,4},{7,5},{8,6},{9,7},{10,8},{11,9},{12,... | collective-permute-start | bytes 3145736 | tf_op jit(solution)/shard_map/ppermute | solution.py:18
  84.4 1.2 copy-start.4
  89.6 39.2 %all-to-all-start.6 = ((bf16[2,128,1024]{2,1,0:T(8,128)(2,1)}), bf16[2,128,1024]{2,1,0:T(8,128)(2,1)S(1)}, u32[]{:S(2)}, u32[]{:S(2)}) async-start(bf16[2,128,1024]{2,1,0:T(8,128)(2,1)} %convert_element_type.59), calls=%async_computation.6 | async-start | bytes 1048576 | tf_op jit(solution)/shard_map/all_to_all | solution.py:161
  128.8 8.9 %all-to-all-start.7 = ((bf16[2,128,512]{2,1,0:T(8,128)(2,1)}), bf16[2,128,512]{2,1,0:T(8,128)(2,1)S(1)}, u32[]{:S(2)}, u32[]{:S(2)}) async-start(bf16[2,128,512]{2,1,0:T(8,128)(2,1)} %add_convert_fusion.2), calls=%async_computation.7 | async-start | bytes 524288 | tf_op jit(solution)/shard_map/all_to_all | solution.py:162
  137.7 8.6 %all-to-all-start.8 = ((bf16[2,128,512]{2,1,0:T(8,128)(2,1)}), bf16[2,128,512]{2,1,0:T(8,128)(2,1)S(1)}, u32[]{:S(2)}, u32[]{:S(2)}) async-start(bf16[2,128,512]{2,1,0:T(8,128)(2,1)} %add_convert_fusion.1), calls=%async_computation.8 | async-start | bytes 524288 | tf_op jit(solution)/shard_map/all_to_all | solution.py:163
where the time goes:
time: 149 us; the launch traced here: 147 us
  waiting for transfers between devices  56.8 us (38%)
  starting transfers between devices  47.1 us (32%)
  local copies, waits for them, and re-layouts  23.5 us (16%)
  other arithmetic  6.48 us (4%)
  blocking collectives  5.24 us (4%)
  matrix products  4.65 us (3%)
  between operations  3.64 us (2%)
    ppermute x6, waiting for transfers between devices, from_behind(): return lax.ppermute(block, axis, route)  32.8 us
    ppermute x6, starting transfers between devices, from_behind(): return lax.ppermute(block, axis, route)  14.9 us
    all_to_all x1, waiting for transfers between devices, per_device(): lax.all_to_all(query_inputs, 'uly', split_axis=1, concat_axis=0, tiled=True)  8.18 us
    all_gather x1, blocking collectives, per_device(): ids_loc = lax.all_gather(segment_ids, 'uly', axis=0, tiled=True)  5.24 us
    all_to_all x1, waiting for transfers between devices, per_device(): lax.all_to_all(key_total, 'uly', split_axis=0, concat_axis=1, tiled=True)  4.72 us
    all_to_all x1, starting transfers between devices, per_device(): lax.all_to_all(lse_parts.reshape(tok_local, -1), 'uly', split_axis=1, con...  4.41 us
    another operation x4, local copies, waits for them, and re-layouts  4.25 us
    unnamed x16, local copies, waits for them, and re-layouts  3.91 us
  transfers between devices with their start and end apart: 15, of which 7 were waited for; matrix products, arithmetic and copies ran while one was open for 22% of the time, Pallas kernels for 0%

commit v1 on v0

v1 whole, which is shorter than its diff:
```python
import functools
import math

import jax
import jax.numpy as jnp
from jax import lax
from jax.experimental import pallas as pl
from jax.experimental.pallas import tpu as pltpu
from jax.sharding import PartitionSpec as P

HEAD_SIZE = 128
QUERY_HEADS = 16
KEY_VALUE_HEADS = 8
GROUP = QUERY_HEADS // KEY_VALUE_HEADS
TILE = 256
FAR = -1e30


def merge_parts(partials):
    highest = jnp.max(partials, axis=-1)
    return highest + jnp.log(jnp.sum(jnp.exp(partials - highest[..., None]), axis=-1))


def row_delta(grad_rows, out_rows):
    row_total = grad_rows.shape[0]
    products = grad_rows.astype(jnp.float32) * out_rows.astype(jnp.float32)
    return jnp.sum(products.reshape(row_total, -1, HEAD_SIZE), axis=-1)


def dot_nt(a, b):
    return lax.dot_general(a, b, (((1,), (1,)), ((), ())), preferred_element_type=jnp.float32)


def dot_nn(a, b):
    return lax.dot_general(a, b, (((1,), (0,)), ((), ())), preferred_element_type=jnp.float32)


def dot_tn(a, b):
    return lax.dot_general(a, b, (((0,), (0,)), ((), ())), preferred_element_type=jnp.float32)


def kernel(
    uly_count, blk_count,
    q_ref, do_ref, k_ref, v_ref, stat_ref, ids_ref,
    dq_ref, dk_ref, dv_ref,
    qb, dob, kvb, statb, idb, bias,
    dqacc, acc0, acc1, acc2, dqs, ret1, ret2, in1, in2, dkvs,
    loc_sem,
    kv_s, kv_r, qd_s, qd_r, st_s, st_r, id_s, id_r,
    h2_s, h2_r, h2i_s, h2i_r, pt_s, pt_r, pti_s, pti_r,
    r1_s, r1_r, r2_s, r2_r, oq_s, oq_r, okv_s, okv_r,
):
    U, B = uly_count, blk_count
    T = q_ref.shape[0]
    R = T * U
    KH = KEY_VALUE_HEADS // U
    D = HEAD_SIZE
    GD = GROUP * D
    scale = 1.0 / math.sqrt(D)
    u = lax.axis_index("uly")
    b = lax.axis_index("blk")
    odd = lax.rem(b, 2)
    even = odd == 0
    mate = b + 1 - 2 * odd

    def at(blk, uly):
        return {"blk": blk, "uly": uly}

    def rcopy(src, dst, ssem, rsem, dev):
        return pltpu.make_async_remote_copy(
            src_ref=src, dst_ref=dst, send_sem=ssem, recv_sem=rsem,
            device_id=dev, device_id_type=pl.DeviceIdType.MESH,
        )

    def cols(first, width):
        return pl.ds(pl.multiple_of(first, 128), width)

    def rows(place):
        return pl.ds(pl.multiple_of(place * T, T), T)

    has_up2 = b + 2 < B
    has_down2 = b >= 2
    sends_mate = jnp.logical_or(even, b >= 3)

    barrier = pltpu.get_barrier_semaphore()
    for k in range(1, U):
        pl.semaphore_signal(
            barrier, inc=1, device_id=at(b, lax.rem(u + k, U)), device_id_type=pl.DeviceIdType.MESH
        )
    pl.semaphore_signal(barrier, inc=1, device_id=at(mate, u), device_id_type=pl.DeviceIdType.MESH)

    @pl.when(has_up2)
    def _():
        pl.semaphore_signal(
            barrier, inc=1, device_id=at(b + 2, u), device_id_type=pl.DeviceIdType.MESH
        )

    @pl.when(has_down2)
    def _():
        pl.semaphore_signal(
            barrier, inc=1, device_id=at(b - 2, u), device_id_type=pl.DeviceIdType.MESH
        )

    expected = U + has_up2.astype(jnp.int32) + has_down2.astype(jnp.int32)
    pl.semaphore_wait(barrier, expected)

    mine = [
        pltpu.make_async_copy(ids_ref, idb.at[0, u], loc_sem.at[0]),
        pltpu.make_async_copy(
            k_ref.at[:, cols(u * KH * D, KH * D)], kvb.at[0, 0, rows(u), :], loc_sem.at[1]
        ),
        pltpu.make_async_copy(
            v_ref.at[:, cols(u * KH * D, KH * D)], kvb.at[0, 1, rows(u), :], loc_sem.at[2]
        ),
        pltpu.make_async_copy(stat_ref.at[u], statb.at[u], loc_sem.at[3]),
        pltpu.make_async_copy(
            q_ref.at[:, cols(u * KH * GD, KH * GD)], qb.at[rows(u), :], loc_sem.at[4]
        ),
        pltpu.make_async_copy(
            do_ref.at[:, cols(u * KH * GD, KH * GD)], dob.at[rows(u), :], loc_sem.at[5]
        ),
    ]
    for copy in mine:
        copy.start()

    def id_in(k, place, dev):
        return rcopy(ids_ref, idb.at[0, place], id_s.at[k - 1], id_r.at[k - 1], dev)

    def st_in(k, place, peer, dev):
        return rcopy(stat_ref.at[peer], statb.at[place], st_s.at[k - 1], st_r.at[k - 1], dev)

    def kv_in(k, which, j, place, peer, dev):
        ref = (k_ref, v_ref)[which]
        return rcopy(
            ref.at[:, cols((peer * KH + j) * D, D)],
            kvb.at[0, which, rows(place), cols(j * D, D)],
            kv_s.at[which, j, k - 1], kv_r.at[which, j, k - 1], dev,
        )

    def qd_in(k, which, j, place, peer, dev):
        ref, buf = ((q_ref, qb), (do_ref, dob))[which]
        return rcopy(
            ref.at[:, cols((peer * KH + j) * GD, GD)],
            buf.at[rows(place), cols(j * GD, GD)],
            qd_s.at[which, j, k - 1], qd_r.at[which, j, k - 1], dev,
        )

    peers = [(k, lax.rem(u + k, U), lax.rem(u + U - k, U)) for k in range(1, U)]
    for k, to, _ in peers:
        id_in(k, u, at(b, to)).start()
    for j in range(KH):
        for k, to, _ in peers:
            for which in range(2):
                kv_in(k, which, j, u, to, at(b, to)).start()
    for k, to, _ in peers:
        st_in(k, u, to, at(b, to)).start()
    for j in range(KH):
        for k, to, _ in peers:
            for which in range(2):
                qd_in(k, which, j, u, to, at(b, to)).start()

    def h2(j):
        return rcopy(
            kvb.at[0, :, :, cols(j * D, D)], kvb.at[2, :, :, cols(j * D, D)],
            h2_s.at[j], h2_r.at[j], at(b + 2, u),
        )

    def h2id():
        return rcopy(idb.at[0], idb.at[2], h2i_s.at[0], h2i_r.at[0], at(b + 2, u))

    def pt(j):
        return rcopy(
            kvb.at[2 * odd, :, :, cols(j * D, D)], kvb.at[1, :, :, cols(j * D, D)],
            pt_s.at[j], pt_r.at[j], at(mate, u),
        )

    def ptid():
        return rcopy(idb.at[2 * odd], idb.at[1], pti_s.at[0], pti_r.at[0], at(mate, u))

    mine[0].wait()
    for k, _, frm in peers:
        id_in(k, frm, at(b, frm)).wait_recv()

    @pl.when(has_up2)
    def _():
        h2id().start()

    @pl.when(even)
    def _():
        ptid().start()

    mine[1].wait()
    mine[2].wait()
    for j in range(KH):
        for k, _, frm in peers:
            for which in range(2):
                kv_in(k, which, j, frm, frm, at(b, frm)).wait_recv()

        @pl.when(has_up2)
        def _():
            h2(j).start()

        @pl.when(even)
        def _():
            pt(j).start()

    def make_bias(hop):
        for kp in range(U):
            key_ids = jnp.broadcast_to(idb[hop, kp, 0:1, :], (T, T)).T
            for qp in range(U):
                query_ids = idb[0, qp, 0:1, :]
                good = key_ids == query_ids
                if hop == 0:
                    kpos = lax.broadcasted_iota(jnp.int32, (T, T), 0) + kp * T
                    qpos = lax.broadcasted_iota(jnp.int32, (T, T), 1) + qp * T
                    good = jnp.logical_and(good, kpos <= qpos)
                bias[hop, kp * T:(kp + 1) * T, qp * T:(qp + 1) * T] = jnp.where(good, 0.0, FAR)

    make_bias(0)

    @pl.when(has_down2)
    def _():
        h2id().wait_recv()
        make_bias(2)

        @pl.when(odd == 1)
        def _():
            ptid().start()

    def arrive2(j):
        @pl.when(has_down2)
        def _():
            h2(j).wait_recv()

            @pl.when(odd == 1)
            def _():
                pt(j).start()

    arrive2(0)

    @pl.when(b >= 1)
    def _():
        ptid().wait_recv()
        make_bias(1)

    for copy in mine[3:]:
        copy.wait()
    for k, _, frm in peers:
        st_in(k, frm, frm, at(b, frm)).wait_recv()

    tile = min(TILE, R)
    steps = R // tile
    per = tile // T if tile >= T else 1

    def stat_row(row, qt):
        parts = [statb[qt * per + i, pl.ds(row, 1), :] for i in range(per)]
        return parts[0] if per == 1 else jnp.concatenate(parts, axis=1)

    G = KH * GROUP

    def hop_grads(hop, j, acc):
        def key_step(kt, _):
            krow = pl.ds(pl.multiple_of(kt * tile, tile), tile)
            kc = kvb[hop, 0, krow, cols(j * D, D)]
            vc = kvb[hop, 1, krow, cols(j * D, D)]

            def query_step(qt, carry):
                dk, dv = carry
                qrow = pl.ds(pl.multiple_of(qt * tile, tile), tile)
                for g in range(GROUP):
                    qc = qb[qrow, cols(j * GD + g * D, D)]
                    dc = dob[qrow, cols(j * GD + g * D, D)]
                    head = j * GROUP + g
                    lse = stat_row(head, qt)
                    delta = stat_row(G + head, qt)
                    w = jnp.exp(dot_nt(kc, qc) * scale - lse + bias[hop, krow, pl.ds(pl.multiple_of(qt * tile, tile), tile)])
                    dv = dv + dot_nn(w.astype(jnp.bfloat16), dc)
                    ds = (w * (dot_nt(vc, dc) - delta)).astype(jnp.bfloat16)
                    dk = dk + dot_nn(ds, qc)
                    part = dot_tn(ds, kc)
                    dqacc[qrow, g * D:(g + 1) * D] += part
                return dk, dv

            zero = jnp.zeros((tile, D), jnp.float32)
            if steps == 1:
                dk, dv = query_step(0, (zero, zero))
            else:
                dk, dv = lax.fori_loop(0, steps, query_step, (zero, zero))
            acc[j, 0, krow, :] = (dk * scale).astype(acc.dtype)
            acc[j, 1, krow, :] = dv.astype(acc.dtype)
            return 0

        if steps == 1:
            key_step(0, 0)
        else:
            lax.fori_loop(0, steps, key_step, 0)

    def give1(j):
        return rcopy(ret1.at[j], in1.at[j], r1_s.at[j], r1_r.at[j], at(mate, u))

    def give2(j):
        return rcopy(ret2.at[j], in2.at[j], r2_s.at[j], r2_r.at[j], at(b - 2, u))

    def oq(k, j, place, dev):
        return rcopy(
            dqs.at[j, rows(place), :], dq_ref.at[:, cols((u * KH + j) * GD, GD)],
            oq_s.at[j, k - 1], oq_r.at[j, k - 1], dev,
        )

    def okv(k, which, j, place, dev):
        ref = (dk_ref, dv_ref)[which]
        return rcopy(
            dkvs.at[j, which, rows(place), :], ref.at[:, cols((u * KH + j) * D, D)],
            okv_s.at[which, j, k - 1], okv_r.at[which, j, k - 1], dev,
        )

    def compute(j):
        for k, _, frm in peers:
            for which in range(2):
                qd_in(k, which, j, frm, frm, at(b, frm)).wait_recv()
        dqacc[...] = jnp.zeros_like(dqacc)
        hop_grads(0, j, acc0)

        @pl.when(has_down2)
        def _():
            hop_grads(2, j, acc2)

        @pl.when(b >= 1)
        def _():
            pt(j).wait_recv()
            hop_grads(1, j, ret1)
            give1(j).start()

        dqs[j] = (dqacc[...] * scale).astype(jnp.bfloat16)
        for k, to, _ in peers:
            oq(k, j, to, at(b, to)).start()
        dq_ref[:, cols((u * KH + j) * GD, GD)] = dqs[j, rows(u), :]

    def stage_a(j):
        @pl.when(jnp.logical_and(odd == 1, has_down2))
        def _():
            give1(j).wait_recv()
            ret2[j] = (acc2[j] + in1[j].astype(jnp.float32)).astype(jnp.bfloat16)

        @pl.when(jnp.logical_and(even, has_down2))
        def _():
            ret2[j] = acc2[j].astype(jnp.bfloat16)

        @pl.when(has_down2)
        def _():
            give2(j).start()

    def stage_b(j):
        @pl.when(even)
        def _():
            give1(j).wait_recv()
            acc0[j] += in1[j].astype(jnp.float32)

        @pl.when(has_up2)
        def _():
            give2(j).wait_recv()
            acc0[j] += in2[j].astype(jnp.float32)

        dkvs[j] = acc0[j].astype(jnp.bfloat16)
        for k, to, _ in peers:
            for which in range(2):
                okv(k, which, j, to, at(b, to)).start()
        for which in range(2):
            ref = (dk_ref, dv_ref)[which]
            ref[:, cols((u * KH + j) * D, D)] = dkvs[j, which, rows(u), :]

    def head_step(j, _):
        @pl.when(j + 1 < KH)
        def _():
            arrive2(jnp.minimum(j + 1, KH - 1))

        compute(j)

        @pl.when(j >= 1)
        def _():
            stage_a(jnp.maximum(j - 1, 0))

        @pl.when(j >= 2)
        def _():
            stage_b(jnp.maximum(j - 2, 0))

        return 0

    lax.fori_loop(0, KH, head_step, 0)
    stage_a(KH - 1)
    if KH >= 2:
        stage_b(KH - 2)
    stage_b(KH - 1)

    for k, to, frm in peers:
        id_in(k, u, at(b, to)).wait_send()
        st_in(k, u, to, at(b, to)).wait_send()

    @pl.when(has_up2)
    def _():
        h2id().wait_send()

    @pl.when(sends_mate)
    def _():
        ptid().wait_send()

    def finish(j, _):
        for k, to, frm in peers:
            for which in range(2):
                kv_in(k, which, j, u, to, at(b, to)).wait_send()
                qd_in(k, which, j, u, to, at(b, to)).wait_send()

        @pl.when(has_up2)
        def _():
            h2(j).wait_send()

        @pl.when(sends_mate)
        def _():
            pt(j).wait_send()

        @pl.when(b >= 1)
        def _():
            give1(j).wait_send()

        @pl.when(has_down2)
        def _():
            give2(j).wait_send()

        for k, to, frm in peers:
            oq(k, j, to, at(b, to)).wait_send()
            for which in range(2):
                okv(k, which, j, to, at(b, to)).wait_send()
            rcopy(
                dqs.at[j, rows(frm), :], dq_ref.at[:, cols((frm * KH + j) * GD, GD)],
                oq_s.at[j, k - 1], oq_r.at[j, k - 1], at(b, frm),
            ).wait_recv()
            for which in range(2):
                ref = (dk_ref, dv_ref)[which]
                rcopy(
                    dkvs.at[j, which, rows(frm), :], ref.at[:, cols((frm * KH + j) * D, D)],
                    okv_s.at[which, j, k - 1], okv_r.at[which, j, k - 1], at(b, frm),
                ).wait_recv()
        return 0

    lax.fori_loop(0, KH, finish, 0)


def per_device(uly_count, blk_count, q, k, v, out, grad, lse_parts, segment_ids):
    U, B = uly_count, blk_count
    T = q.shape[0]
    R = T * U
    KH = KEY_VALUE_HEADS // U
    G = KH * GROUP
    D = HEAD_SIZE
    lse = merge_parts(lse_parts).T.reshape(U, G, T)
    delta = row_delta(grad, out).T.reshape(U, G, T)
    stat_rows = -(-2 * G // 8) * 8
    stat = jnp.concatenate([lse, delta], axis=1)
    stat = jnp.pad(stat, ((0, 0), (0, stat_rows - 2 * G), (0, 0)))
    ids = jnp.broadcast_to(segment_ids.astype(jnp.float32)[None, :], (8, T))
    bf, f32 = jnp.bfloat16, jnp.float32
    n = max(U - 1, 1)
    dma = pltpu.SemaphoreType.DMA
    sems = []
    for shape in [(2, KH, n), (2, KH, n), (n,), (n,), (KH,), (1,), (KH,), (1,), (KH,), (KH,), (KH, n), (2, KH, n)]:
        sems += [dma(shape), dma(shape)]
    vm = pltpu.VMEM
    return pl.pallas_call(
        functools.partial(kernel, U, B),
        out_shape=(
            jax.ShapeDtypeStruct(q.shape, bf),
            jax.ShapeDtypeStruct(k.shape, bf),
            jax.ShapeDtypeStruct(v.shape, bf),
        ),
        in_specs=[pl.BlockSpec(memory_space=vm)] * 6,
        out_specs=tuple([pl.BlockSpec(memory_space=vm)] * 3),
        scratch_shapes=[
            vm((R, G * D), bf),
            vm((R, G * D), bf),
            vm((3, 2, R, KH * D), bf),
            vm((U, stat_rows, T), f32),
            vm((3, U, 8, T), f32),
            vm((3, R, R), f32),
            vm((R, GROUP * D), f32),
            vm((KH, 2, R, D), f32),
            vm((8, 128), f32),
            vm((KH, 2, R, D), f32),
            vm((KH, R, GROUP * D), bf),
            vm((KH, 2, R, D), bf),
            vm((KH, 2, R, D), bf),
            vm((KH, 2, R, D), bf),
            vm((KH, 2, R, D), bf),
            vm((KH, 2, R, D), bf),
            dma((6,)),
        ] + sems,
        compiler_params=pltpu.CompilerParams(
            collective_id=0, has_side_effects=True, vmem_limit_bytes=56 * 1024 * 1024
        ),
    )(q, grad, k, v, stat, ids)


def solution(mesh):
    spec = P(("blk", "uly"), None)
    body = functools.partial(per_device, mesh.shape["uly"], mesh.shape["blk"])
    return jax.shard_map(
        body,
        mesh=mesh,
        in_specs=(spec, spec, spec, spec, spec, P(("blk", "uly"), None, None), P(("blk", "uly"))),
        out_specs=(spec, spec, spec),
        check_vma=False,
    )
```

time: 149 us -> 51 us (0.34)
  waiting for transfers between devices: 56.8 us -> 0 us
  starting transfers between devices: 47.1 us -> 0 us
  Pallas kernels: 0 us -> 42.5 us
  local copies, waits for them, and re-layouts: 23.5 us -> 5.21 us
  blocking collectives: 5.24 us -> 0 us
  matrix products: 4.65 us -> 0 us
  other arithmetic: 6.48 us -> 2.35 us
  between operations: 3.64 us -> 0.71 us
    pallas_call x0 -> x1, Pallas kernels: none -> 42.5 us  [per_device(): pl.pallas_call(functools.partial(kernel, U, B), out_shape=(jax.ShapeDtype...]
    ppermute x6 -> x0, waiting for transfers between devices: 32.8 us -> none  [from_behind(): return lax.ppermute(block, axis, route)]
    all_to_all x9 -> x0, starting transfers between devices: 32.1 us -> none  [the longest x1 4.41 us: per_device(): lax.all_to_all(lse_parts.reshape(tok_local, -1), 'uly', split_axis=1, con...]
    all_to_all x9 -> x0, waiting for transfers between devices: 24 us -> none  [the longest x1 8.18 us: per_device(): lax.all_to_all(query_inputs, 'uly', split_axis=1, concat_axis=0, tiled=True)]
    ppermute x6 -> x0, starting transfers between devices: 14.9 us -> none  [from_behind(): return lax.ppermute(block, axis, route)]
    all_to_all x9 -> x0, local copies, waits for them, and re-layouts: 6.58 us -> none  [the longest x1 1.73 us: per_device(): lax.all_to_all(value_inputs, 'uly', split_axis=1, concat_axis=0, tiled=True)]
    all_gather x1 -> x0, blocking collectives: 5.24 us -> none  [per_device(): ids_loc = lax.all_gather(segment_ids, 'uly', axis=0, tiled=True)]
    dot_general x5 -> x0, matrix products: 4.65 us -> none  [the longest x1 1.64 us: tile_grads(): jnp.einsum('hgmn,mhgd->nhd', score_grad, query_blk, preferred_element_typ...]
  transfers between devices with their start and end apart: 15 -> 0, of which waited for: 7 -> 0; matrix products, arithmetic and copies ran while one was open for 22% -> 0% of each run, Pallas kernels for 0% -> 0%
where the time goes in v1:
time: 51 us; the launch traced here: 50.8 us
  Pallas kernels  42.5 us (83%)
  local copies, waits for them, and re-layouts  5.21 us (10%)
  other arithmetic  2.35 us (5%)
  between operations  0.71 us (1%)
    pallas_call x1, Pallas kernels, per_device(): pl.pallas_call(functools.partial(kernel, U, B), out_shape=(jax.ShapeDtype...  42.5 us
    unnamed x12, local copies, waits for them, and re-layouts  4.56 us
    unnamed x1, other arithmetic  1.33 us

profile of v1, /device:TPU:0, one launch (start us, length us, event | category | flops | bytes accessed | tf_op | source)
XLA Modules:
  0.0 50.8 jit_solution(4132601552195030193)
XLA Ops:
  0.6 1.3 %multiply_bitcast_fusion = f32[16,8,16,128]{3,1,2,0:T(8,128)S(1)} fusion(bf16[128,2048]{1,0:T(8,128)(2,1)} %param.10, bf16[128,2048]{1,0:T(8,128)(2,1)} %do_ref.1), kind=kLoop, calls=%fused_computation | loop fusion | flops 786432 | bytes 2097152
  2.0 0.2 copy.11
  2.2 0.3 reduce_sum.19
  2.5 0.0 copy-start.2
  2.5 0.1 copy.10
  2.6 0.7 %copy-done.2 = f32[128,16,2]{0,2,1:T(2,128)S(1)} copy-done((f32[128,16,2]{0,2,1:T(2,128)S(1)}, f32[128,16,2]{0,2,1:T(2,128)}, u32[]{:S(2)}) %copy-start.2) | copy-done | bytes 16408
  3.3 0.0 copy-start.3
  3.3 0.6 %pad_maximum_fusion.stat_ref = f32[2,16,128]{2,1,0:T(8,128)} fusion(f32[2,8,128]{2,1,0:T(8,128)S(1)} %bitcast.11, f32[2,8,128]{2,1,0:T(8,128)S(1)} %add_bitcast_fusion), kind=kLoop, calls=%fused_computation.1 | loop fusion | flops 4096 | bytes 32768 | tf_op jit(solution)/shard_map/concatenate | solution.py:458
  3.9 0.0 copy-done.3
  4.0 0.6 %broadcast_in_dim.2.ids_ref = f32[8,128]{1,0:T(8,128)} broadcast(f32[128]{0:T(128)S(1)} %convert_element_type.11), dimensions={1} | broadcast | bytes 4608 | tf_op jit(solution)/shard_map/broadcast_in_dim | solution.py:460
  4.6 42.5 %shard_map.94 = (bf16[128,2048]{1,0:T(8,128)(2,1)}, bf16[128,1024]{1,0:T(8,128)(2,1)}, bf16[128,1024]{1,0:T(8,128)(2,1)}) custom-call(bf16[128,2048]{1,0:T(8,128)(2,1)} %q_ref.1, bf16[128,2048]{1,0:T(8,128)(2,1)} %do_ref.1, bf16[128,1024]{1,0:T(8,128)(2,1)} %k_ref.1, bf16[128,1024]{1,0:T(8,128)(2,1)} %v_ref.1, f32[2,16,128]{2,1,0:T(8,128)} %pad_maximum_fusion.stat_ref, ...), custom_call_target="tpu_custom_call" | custom-call | tf_op jit(solution)/shard_map/pallas_call | solution.py:468
  47.1 0.0 copy-start.1
  47.1 1.9 %copy.15 = bf16[128,2048]{1,0:T(8,128)(2,1)} copy(bf16[128,2048]{1,0:T(8,128)(2,1)} %get-tuple-element.6) | data formatting | bytes 1048576
  49.0 0.0 copy-done.1
  49.0 0.0 copy-start
  49.0 0.7 %copy.16 = bf16[128,1024]{1,0:T(8,128)(2,1)} copy(bf16[128,1024]{1,0:T(8,128)(2,1)S(1)} %copy-done.1) | data formatting | bytes 524288
  49.7 0.3 copy-done
  50.1 0.7 %copy.17 = bf16[128,1024]{1,0:T(8,128)(2,1)} copy(bf16[128,1024]{1,0:T(8,128)(2,1)S(1)} %copy-done) | data formatting | bytes 524288
  (4 shorter events, 0.1 us)
Async XLA Ops:
  2.5 0.7 %copy-start.2 = (f32[128,16,2]{0,2,1:T(2,128)S(1)}, f32[128,16,2]{0,2,1:T(2,128)}, u32[]{:S(2)}) copy-start(f32[128,16,2]{0,2,1:T(2,128)} %param.12) | copy-start | bytes 49156
  3.3 0.7 %copy-start.3 = (s32[128]{0:T(128)S(1)}, s32[128]{0:T(128)}, u32[]{:S(2)}) copy-start(s32[128]{0:T(128)} %param.13) | copy-start | bytes 1540
  47.1 1.9 %copy-start.1 = (bf16[128,1024]{1,0:T(8,128)(2,1)S(1)}, bf16[128,1024]{1,0:T(8,128)(2,1)}, u32[]{:S(2)}) copy-start(bf16[128,1024]{1,0:T(8,128)(2,1)} %get-tuple-element.7) | copy-start | bytes 786436
  49.0 1.0 %copy-start = (bf16[128,1024]{1,0:T(8,128)(2,1)S(1)}, bf16[128,1024]{1,0:T(8,128)(2,1)}, u32[]{:S(2)}) copy-start(bf16[128,1024]{1,0:T(8,128)(2,1)} %get-tuple-element.8) | copy-start | bytes 786436

commit v2 on v1

--- a/solution.py
+++ b/solution.py
@@ -16,17 +16,6 @@
 FAR = -1e30
 
 
-def merge_parts(partials):
-    highest = jnp.max(partials, axis=-1)
-    return highest + jnp.log(jnp.sum(jnp.exp(partials - highest[..., None]), axis=-1))
-
-
-def row_delta(grad_rows, out_rows):
-    row_total = grad_rows.shape[0]
-    products = grad_rows.astype(jnp.float32) * out_rows.astype(jnp.float32)
-    return jnp.sum(products.reshape(row_total, -1, HEAD_SIZE), axis=-1)
-
-
 def dot_nt(a, b):
     return lax.dot_general(a, b, (((1,), (1,)), ((), ())), preferred_element_type=jnp.float32)
 
@@ -41,10 +30,11 @@
 
 def kernel(
     uly_count, blk_count,
-    q_ref, do_ref, k_ref, v_ref, stat_ref, ids_ref,
+    q_ref, do_hbm, k_hbm, v_hbm, out_hbm, lp_hbm, ids_hbm,
     dq_ref, dk_ref, dv_ref,
     qb, dob, kvb, statb, idb, bias,
-    dqacc, acc0, acc1, acc2, dqs, ret1, ret2, in1, in2, dkvs,
+    dqacc, acc0, acc2, dqs, ret1, ret2, in1, in2, dkvs,
+    do_ref, k_ref, v_ref, out_ref, lp_ref, ids_ref, stat_ref,
     loc_sem,
     kv_s, kv_r, qd_s, qd_r, st_s, st_r, id_s, id_r,
     h2_s, h2_r, h2i_s, h2i_r, pt_s, pt_r, pti_s, pti_r,
@@ -82,6 +72,16 @@
     has_down2 = b >= 2
     sends_mate = jnp.logical_or(even, b >= 3)
 
+    loads = [
+        pltpu.make_async_copy(src, dst, loc_sem.at[5 + i])
+        for i, (src, dst) in enumerate([
+            (ids_hbm, ids_ref), (k_hbm, k_ref), (v_hbm, v_ref),
+            (do_hbm, do_ref), (out_hbm, out_ref), (lp_hbm, lp_ref),
+        ])
+    ]
+    for copy in loads:
+        copy.start()
+
     barrier = pltpu.get_barrier_semaphore()
     for k in range(1, U):
         pl.semaphore_signal(
@@ -104,24 +104,23 @@
     expected = U + has_up2.astype(jnp.int32) + has_down2.astype(jnp.int32)
     pl.semaphore_wait(barrier, expected)
 
-    mine = [
-        pltpu.make_async_copy(ids_ref, idb.at[0, u], loc_sem.at[0]),
+    own_q = [
         pltpu.make_async_copy(
-            k_ref.at[:, cols(u * KH * D, KH * D)], kvb.at[0, 0, rows(u), :], loc_sem.at[1]
+            q_ref.at[:, cols(u * KH * GD, KH * GD)], qb.at[rows(u), :], loc_sem.at[0]
         ),
         pltpu.make_async_copy(
-            v_ref.at[:, cols(u * KH * D, KH * D)], kvb.at[0, 1, rows(u), :], loc_sem.at[2]
+            do_hbm.at[:, cols(u * KH * GD, KH * GD)], dob.at[rows(u), :], loc_sem.at[1]
         ),
-        pltpu.make_async_copy(stat_ref.at[u], statb.at[u], loc_sem.at[3]),
+    ]
+    own_kv = [
         pltpu.make_async_copy(
-            q_ref.at[:, cols(u * KH * GD, KH * GD)], qb.at[rows(u), :], loc_sem.at[4]
+            k_hbm.at[:, cols(u * KH * D, KH * D)], kvb.at[0, 0, rows(u), :], loc_sem.at[2]
         ),
         pltpu.make_async_copy(
-            do_ref.at[:, cols(u * KH * GD, KH * GD)], dob.at[rows(u), :], loc_sem.at[5]
+            v_hbm.at[:, cols(u * KH * D, KH * D)], kvb.at[0, 1, rows(u), :], loc_sem.at[3]
         ),
     ]
-    for copy in mine:
-        copy.start()
+    own_id = pltpu.make_async_copy(ids_hbm, idb.at[0, u], loc_sem.at[4])
 
     def id_in(k, place, dev):
         return rcopy(ids_ref, idb.at[0, place], id_s.at[k - 1], id_r.at[k - 1], dev)
@@ -146,18 +145,46 @@
         )
 
     peers = [(k, lax.rem(u + k, U), lax.rem(u + U - k, U)) for k in range(1, U)]
+    loads[0].wait()
     for k, to, _ in peers:
         id_in(k, u, at(b, to)).start()
+    loads[1].wait()
+    loads[2].wait()
     for j in range(KH):
         for k, to, _ in peers:
             for which in range(2):
                 kv_in(k, which, j, u, to, at(b, to)).start()
-    for k, to, _ in peers:
-        st_in(k, u, to, at(b, to)).start()
+    for copy in [own_id] + own_kv + own_q:
+        copy.start()
+
+    for copy in loads[3:]:
+        copy.wait()
+    G = KH * GROUP
+    lane = lax.broadcasted_iota(jnp.int32, (T, 128), 1)
+    table = jnp.zeros((T, 128), jnp.float32)
+    for h in range(U * G):
+        piece = slice(h * D, (h + 1) * D)
+        total = jnp.sum(
+            do_ref[:, piece].astype(jnp.float32) * out_ref[:, piece].astype(jnp.float32),
+            axis=1, keepdims=True,
+        )
+        table = jnp.where(lane == h, total, table)
+    table = table.T
+    part0, part1 = lp_ref[:, 0, :], lp_ref[:, 1, :]
+    highest = jnp.maximum(part0, part1)
+    lse_rows = highest + jnp.log(jnp.exp(part0 - highest) + jnp.exp(part1 - highest))
+    for p in range(U):
+        stat_ref[p, :G, :] = lse_rows[p * G:(p + 1) * G]
+        stat_ref[p, G:2 * G, :] = table[p * G:(p + 1) * G]
+    statb[u] = stat_ref[u]
+
     for j in range(KH):
         for k, to, _ in peers:
             for which in range(2):
                 qd_in(k, which, j, u, to, at(b, to)).start()
+        if j == 0:
+            for k, to, _ in peers:
+                st_in(k, u, to, at(b, to)).start()
 
     def h2(j):
         return rcopy(
@@ -177,7 +204,7 @@
     def ptid():
         return rcopy(idb.at[2 * odd], idb.at[1], pti_s.at[0], pti_r.at[0], at(mate, u))
 
-    mine[0].wait()
+    own_id.wait()
     for k, _, frm in peers:
         id_in(k, frm, at(b, frm)).wait_recv()
 
@@ -189,8 +216,8 @@
     def _():
         ptid().start()
 
-    mine[1].wait()
-    mine[2].wait()
+    for copy in own_kv:
+        copy.wait()
     for j in range(KH):
         for k, _, frm in peers:
             for which in range(2):
@@ -206,9 +233,9 @@
 
     def make_bias(hop):
         for kp in range(U):
-            key_ids = jnp.broadcast_to(idb[hop, kp, 0:1, :], (T, T)).T
+            key_ids = jnp.broadcast_to(idb[hop, kp, 0:1, :].astype(jnp.float32), (T, T)).T
             for qp in range(U):
-                query_ids = idb[0, qp, 0:1, :]
+                query_ids = idb[0, qp, 0:1, :].astype(jnp.float32)
                 good = key_ids == query_ids
                 if hop == 0:
                     kpos = lax.broadcasted_iota(jnp.int32, (T, T), 0) + kp * T
@@ -243,7 +270,7 @@
         ptid().wait_recv()
         make_bias(1)
 
-    for copy in mine[3:]:
+    for copy in own_q:
         copy.wait()
     for k, _, frm in peers:
         st_in(k, frm, frm, at(b, frm)).wait_recv()
@@ -255,8 +282,6 @@
     def stat_row(row, qt):
         parts = [statb[qt * per + i, pl.ds(row, 1), :] for i in range(per)]
         return parts[0] if per == 1 else jnp.concatenate(parts, axis=1)
-
-    G = KH * GROUP
 
     def hop_grads(hop, j, acc):
         def key_step(kt, _):
@@ -319,17 +344,19 @@
             for which in range(2):
                 qd_in(k, which, j, frm, frm, at(b, frm)).wait_recv()
         dqacc[...] = jnp.zeros_like(dqacc)
-        hop_grads(0, j, acc0)
-
-        @pl.when(has_down2)
-        def _():
-            hop_grads(2, j, acc2)
 
         @pl.when(b >= 1)
         def _():
             pt(j).wait_recv()
             hop_grads(1, j, ret1)
             give1(j).start()
+
+        @pl.when(has_down2)
+        def _():
+            hop_grads(2, j, acc2)
+
+        stage_a(j)
+        hop_grads(0, j, acc0)
 
         dqs[j] = (dqacc[...] * scale).astype(jnp.bfloat16)
         for k, to, _ in peers:
@@ -376,10 +403,6 @@
 
         compute(j)
 
-        @pl.when(j >= 1)
-        def _():
-            stage_a(jnp.maximum(j - 1, 0))
-
         @pl.when(j >= 2)
         def _():
             stage_b(jnp.maximum(j - 2, 0))
@@ -387,7 +410,6 @@
         return 0
 
     lax.fori_loop(0, KH, head_step, 0)
-    stage_a(KH - 1)
     if KH >= 2:
         stage_b(KH - 2)
     stage_b(KH - 1)
@@ -452,12 +474,9 @@
     KH = KEY_VALUE_HEADS // U
     G = KH * GROUP
     D = HEAD_SIZE
-    lse = merge_parts(lse_parts).T.reshape(U, G, T)
-    delta = row_delta(grad, out).T.reshape(U, G, T)
     stat_rows = -(-2 * G // 8) * 8
-    stat = jnp.concatenate([lse, delta], axis=1)
-    stat = jnp.pad(stat, ((0, 0), (0, stat_rows - 2 * G), (0, 0)))
-    ids = jnp.broadcast_to(segment_ids.astype(jnp.float32)[None, :], (8, T))
+    parts = lse_parts.transpose(1, 2, 0)
+    ids = segment_ids.reshape(1, T)
     bf, f32 = jnp.bfloat16, jnp.float32
     n = max(U - 1, 1)
     dma = pltpu.SemaphoreType.DMA
@@ -472,18 +491,17 @@
             jax.ShapeDtypeStruct(k.shape, bf),
             jax.ShapeDtypeStruct(v.shape, bf),
         ),
-        in_specs=[pl.BlockSpec(memory_space=vm)] * 6,
+        in_specs=[pl.BlockSpec(memory_space=pltpu.HBM)] * 7,
         out_specs=tuple([pl.BlockSpec(memory_space=vm)] * 3),
         scratch_shapes=[
             vm((R, G * D), bf),
             vm((R, G * D), bf),
             vm((3, 2, R, KH * D), bf),
             vm((U, stat_rows, T), f32),
-            vm((3, U, 8, T), f32),
+            vm((3, U, 1, T), jnp.int32),
             vm((3, R, R), f32),
             vm((R, GROUP * D), f32),
             vm((KH, 2, R, D), f32),
-            vm((8, 128), f32),
             vm((KH, 2, R, D), f32),
             vm((KH, R, GROUP * D), bf),
             vm((KH, 2, R, D), bf),
@@ -491,12 +509,19 @@
             vm((KH, 2, R, D), bf),
             vm((KH, 2, R, D), bf),
             vm((KH, 2, R, D), bf),
-            dma((6,)),
+            vm(q.shape, bf),
+            vm(k.shape, bf),
+            vm(v.shape, bf),
+            vm(q.shape, bf),
+            vm(parts.shape, f32),
+            vm((1, T), jnp.int32),
+            vm((U, stat_rows, T), f32),
+            dma((11,)),
         ] + sems,
         compiler_params=pltpu.CompilerParams(
-            collective_id=0, has_side_effects=True, vmem_limit_bytes=56 * 1024 * 1024
+            collective_id=0, has_side_effects=True, vmem_limit_bytes=56 << 20
         ),
-    )(q, grad, k, v, stat, ids)
+    )(q, grad, k, v, out, parts, ids)
 
 
 def solution(mesh):

time: 51 us -> 40.4 us (0.79)
  Pallas kernels: 42.5 us -> 35.9 us
  other arithmetic: 2.35 us -> 0 us
  local copies, waits for them, and re-layouts: 5.21 us -> 3.67 us
    pallas_call x1, Pallas kernels: 42.5 us -> 35.9 us  [per_device(): pl.pallas_call(functools.partial(kernel, U, B), out_shape=(jax.ShapeDtype...]
    unnamed x1 -> x0, other arithmetic: 1.33 us -> none
    unnamed x12 -> x7, local copies, waits for them, and re-layouts: 4.56 us -> 3.67 us
    concatenate x1 -> x0, other arithmetic: 0.61 us -> none  [per_device(): stat = jnp.concatenate([lse, delta], axis=1)]
    broadcast_in_dim x1 -> x0, local copies, waits for them, and re-layouts: 0.6 us -> none  [per_device(): ids = jnp.broadcast_to(segment_ids.astype(jnp.float32)[None, :], (8, T))]
where the time goes in v2:
time: 40.4 us; the launch traced here: 40.2 us
  Pallas kernels  35.9 us (89%)
  local copies, waits for them, and re-layouts  3.67 us (9%)
  between operations  0.65 us (2%)
    pallas_call x1, Pallas kernels, per_device(): pl.pallas_call(functools.partial(kernel, U, B), out_shape=(jax.ShapeDtype...  35.9 us
    unnamed x7, local copies, waits for them, and re-layouts  3.67 us

profile of v2, /device:TPU:0, one launch (start us, length us, event | category | flops | bytes accessed | tf_op | source)
XLA Modules:
  0.0 40.2 jit_solution(11293139002810266084)
XLA Ops:
  0.6 35.9 %shard_map.94 = (bf16[128,2048]{1,0:T(8,128)(2,1)}, bf16[128,1024]{1,0:T(8,128)(2,1)}, bf16[128,1024]{1,0:T(8,128)(2,1)}) custom-call(bf16[128,2048]{1,0:T(8,128)(2,1)} %q_ref.1, bf16[128,2048]{1,0:T(8,128)(2,1)} %do_hbm.1, bf16[128,1024]{1,0:T(8,128)(2,1)} %k_hbm.1, bf16[128,1024]{1,0:T(8,128)(2,1)} %v_hbm.1, bf16[128,2048]{1,0:T(8,128)(2,1)} %out_hbm.1, ...), custom_call_target="tpu_custom_call" | custom-call | tf_op jit(solution)/shard_map/pallas_call | solution.py:487
  36.5 0.0 copy-start.1
  36.5 1.9 %copy.13 = bf16[128,2048]{1,0:T(8,128)(2,1)} copy(bf16[128,2048]{1,0:T(8,128)(2,1)} %get-tuple-element.6) | data formatting | bytes 1048576
  38.4 0.0 copy-done.1
  38.5 0.0 copy-start
  38.5 0.7 %copy.14 = bf16[128,1024]{1,0:T(8,128)(2,1)} copy(bf16[128,1024]{1,0:T(8,128)(2,1)S(1)} %copy-done.1) | data formatting | bytes 524288
  39.2 0.3 copy-done
  39.5 0.7 %copy.15 = bf16[128,1024]{1,0:T(8,128)(2,1)} copy(bf16[128,1024]{1,0:T(8,128)(2,1)S(1)} %copy-done) | data formatting | bytes 524288
Async XLA Ops:
  36.5 1.9 %copy-start.1 = (bf16[128,1024]{1,0:T(8,128)(2,1)S(1)}, bf16[128,1024]{1,0:T(8,128)(2,1)}, u32[]{:S(2)}) copy-start(bf16[128,1024]{1,0:T(8,128)(2,1)} %get-tuple-element.7) | copy-start | bytes 786436
  38.5 1.0 %copy-start = (bf16[128,1024]{1,0:T(8,128)(2,1)S(1)}, bf16[128,1024]{1,0:T(8,128)(2,1)}, u32[]{:S(2)}) copy-start(bf16[128,1024]{1,0:T(8,128)(2,1)} %get-tuple-element.8) | copy-start | bytes 786436

commit v3 on v2

--- a/solution.py
+++ b/solution.py
@@ -13,6 +13,7 @@
 KEY_VALUE_HEADS = 8
 GROUP = QUERY_HEADS // KEY_VALUE_HEADS
 TILE = 256
+PIECES = 2
 FAR = -1e30
 
 
@@ -35,7 +36,7 @@
     qb, dob, kvb, statb, idb, bias,
     dqacc, acc0, acc2, dqs, ret1, ret2, in1, in2, dkvs,
     do_ref, k_ref, v_ref, out_ref, lp_ref, ids_ref, stat_ref,
-    loc_sem,
+    loc_sem, keep_sem,
     kv_s, kv_r, qd_s, qd_r, st_s, st_r, id_s, id_r,
     h2_s, h2_r, h2i_s, h2i_r, pt_s, pt_r, pti_s, pti_r,
     r1_s, r1_r, r2_s, r2_r, oq_s, oq_r, okv_s, okv_r,
@@ -339,6 +340,18 @@
             okv_s.at[which, j, k - 1], okv_r.at[which, j, k - 1], dev,
         )
 
+    def keep_q(j):
+        return pltpu.make_async_copy(
+            dqs.at[j, rows(u), :], dq_ref.at[:, cols((u * KH + j) * GD, GD)], keep_sem.at[2, j]
+        )
+
+    def keep_kv(which, j):
+        ref = (dk_ref, dv_ref)[which]
+        return pltpu.make_async_copy(
+            dkvs.at[j, which, rows(u), :], ref.at[:, cols((u * KH + j) * D, D)],
+            keep_sem.at[which, j],
+        )
+
     def compute(j):
         for k, _, frm in peers:
             for which in range(2):
@@ -361,7 +374,7 @@
         dqs[j] = (dqacc[...] * scale).astype(jnp.bfloat16)
         for k, to, _ in peers:
             oq(k, j, to, at(b, to)).start()
-        dq_ref[:, cols((u * KH + j) * GD, GD)] = dqs[j, rows(u), :]
+        keep_q(j).start()
 
     def stage_a(j):
         @pl.when(jnp.logical_and(odd == 1, has_down2))
@@ -393,8 +406,7 @@
             for which in range(2):
                 okv(k, which, j, to, at(b, to)).start()
         for which in range(2):
-            ref = (dk_ref, dv_ref)[which]
-            ref[:, cols((u * KH + j) * D, D)] = dkvs[j, which, rows(u), :]
+            keep_kv(which, j).start()
 
     def head_step(j, _):
         @pl.when(j + 1 < KH)
@@ -427,6 +439,9 @@
         ptid().wait_send()
 
     def finish(j, _):
+        keep_q(j).wait()
+        for which in range(2):
+            keep_kv(which, j).wait()
         for k, to, frm in peers:
             for which in range(2):
                 kv_in(k, which, j, u, to, at(b, to)).wait_send()
@@ -465,6 +480,27 @@
         return 0
 
     lax.fori_loop(0, KH, finish, 0)
+
+
+def close_kernel(a_in, b_in, c_in, a_out, b_out, c_out, a_mid, b_mid, c_mid, in_sem, out_sem):
+    moves = []
+    for i, (src, mid, dst) in enumerate(
+        [(a_in, a_mid, a_out), (b_in, b_mid, b_out), (c_in, c_mid, c_out)]
+    ):
+        height = src.shape[0] // PIECES
+        for n in range(PIECES):
+            part = pl.ds(n * height, height)
+            moves.append((
+                pltpu.make_async_copy(src.at[part], mid.at[part], in_sem.at[i, n]),
+                pltpu.make_async_copy(mid.at[part], dst.at[part], out_sem.at[i, n]),
+            ))
+    for load, _ in moves:
+        load.start()
+    for load, store in moves:
+        load.wait()
+        store.start()
+    for _, store in moves:
+        store.wait()
 
 
 def per_device(uly_count, blk_count, q, k, v, out, grad, lse_parts, segment_ids):
@@ -484,7 +520,7 @@
     for shape in [(2, KH, n), (2, KH, n), (n,), (n,), (KH,), (1,), (KH,), (1,), (KH,), (KH,), (KH, n), (2, KH, n)]:
         sems += [dma(shape), dma(shape)]
     vm = pltpu.VMEM
-    return pl.pallas_call(
+    results = pl.pallas_call(
         functools.partial(kernel, U, B),
         out_shape=(
             jax.ShapeDtypeStruct(q.shape, bf),
@@ -492,7 +528,7 @@
             jax.ShapeDtypeStruct(v.shape, bf),
         ),
         in_specs=[pl.BlockSpec(memory_space=pltpu.HBM)] * 7,
-        out_specs=tuple([pl.BlockSpec(memory_space=vm)] * 3),
+        out_specs=tuple([pl.BlockSpec(memory_space=pltpu.HBM)] * 3),
         scratch_shapes=[
             vm((R, G * D), bf),
             vm((R, G * D), bf),
@@ -517,11 +553,22 @@
             vm((1, T), jnp.int32),
             vm((U, stat_rows, T), f32),
             dma((11,)),
+            dma((3, KH)),
         ] + sems,
         compiler_params=pltpu.CompilerParams(
             collective_id=0, has_side_effects=True, vmem_limit_bytes=56 << 20
         ),
     )(q, grad, k, v, out, parts, ids)
+    hbm = [pl.BlockSpec(memory_space=pltpu.HBM)] * 3
+    return pl.pallas_call(
+        close_kernel,
+        out_shape=tuple(jax.ShapeDtypeStruct(r.shape, r.dtype) for r in results),
+        in_specs=hbm,
+        out_specs=tuple(hbm),
+        scratch_shapes=[vm(r.shape, r.dtype) for r in results]
+        + [dma((3, PIECES)), dma((3, PIECES))],
+        compiler_params=pltpu.CompilerParams(vmem_limit_bytes=56 << 20),
+    )(*results)
 
 
 def solution(mesh):

time: 40.4 us -> 37.9 us (0.938)
  local copies, waits for them, and re-layouts: 3.67 us -> 0 us
  Pallas kernels: 35.9 us -> 37.1 us
    unnamed x7 -> x0, local copies, waits for them, and re-layouts: 3.67 us -> none
    pallas_call x0 -> x1, Pallas kernels: none -> 2.01 us  [per_device(): pl.pallas_call(close_kernel, out_shape=tuple((jax.ShapeDtypeStruct(r.shap...]
    pallas_call x1, Pallas kernels: 35.9 us -> 35.1 us  [per_device(): pl.pallas_call(functools.partial(kernel, U, B), out_shape=(jax.ShapeDtype...]
where the time goes in v3:
time: 37.9 us; the launch traced here: 37.8 us
  Pallas kernels  37.1 us (98%)
  between operations  0.64 us (2%)
    pallas_call x1, Pallas kernels, per_device(): pl.pallas_call(functools.partial(kernel, U, B), out_shape=(jax.ShapeDtype...  35.1 us
    pallas_call x1, Pallas kernels, per_device(): pl.pallas_call(close_kernel, out_shape=tuple((jax.ShapeDtypeStruct(r.shap...  2.01 us

profile of v3, /device:TPU:0, one launch (start us, length us, event | category | flops | bytes accessed | tf_op | source)
XLA Modules:
  0.0 37.8 jit_solution(6978565182788873400)
XLA Ops:
  0.6 35.1 %shard_map.94 = (bf16[128,2048]{1,0:T(8,128)(2,1)}, bf16[128,1024]{1,0:T(8,128)(2,1)}, bf16[128,1024]{1,0:T(8,128)(2,1)}) custom-call(bf16[128,2048]{1,0:T(8,128)(2,1)} %q_ref.1, bf16[128,2048]{1,0:T(8,128)(2,1)} %do_hbm.1, bf16[128,1024]{1,0:T(8,128)(2,1)} %k_hbm.1, bf16[128,1024]{1,0:T(8,128)(2,1)} %v_hbm.1, bf16[128,2048]{1,0:T(8,128)(2,1)} %out_hbm.1, ...), custom_call_target="tpu_custom_call" | custom-call | tf_op jit(solution)/shard_map/pallas_call | solution.py:523
  35.7 2.0 %shard_map.95 = (bf16[128,2048]{1,0:T(8,128)(2,1)}, bf16[128,1024]{1,0:T(8,128)(2,1)}, bf16[128,1024]{1,0:T(8,128)(2,1)}) custom-call(bf16[128,2048]{1,0:T(8,128)(2,1)} %get-tuple-element.6.a_in, bf16[128,1024]{1,0:T(8,128)(2,1)} %get-tuple-element.7.b_in, bf16[128,1024]{1,0:T(8,128)(2,1)} %get-tuple-element.8.c_in), custom_call_target="tpu_custom_call" | custom-call | tf_op jit(solution)/shard_map/pallas_call | solution.py:563

commit v4 on v3

--- a/solution.py
+++ b/solution.py
@@ -80,7 +80,15 @@
             (do_hbm, do_ref), (out_hbm, out_ref), (lp_hbm, lp_ref),
         ])
     ]
-    for copy in loads:
+    own_kv = [
+        pltpu.make_async_copy(
+            k_hbm.at[:, cols(u * KH * D, KH * D)], kvb.at[0, 0, rows(u), :], loc_sem.at[2]
+        ),
+        pltpu.make_async_copy(
+            v_hbm.at[:, cols(u * KH * D, KH * D)], kvb.at[0, 1, rows(u), :], loc_sem.at[3]
+        ),
+    ]
+    for copy in own_kv + loads:
         copy.start()
 
     barrier = pltpu.get_barrier_semaphore()
@@ -113,14 +121,6 @@
             do_hbm.at[:, cols(u * KH * GD, KH * GD)], dob.at[rows(u), :], loc_sem.at[1]
         ),
     ]
-    own_kv = [
-        pltpu.make_async_copy(
-            k_hbm.at[:, cols(u * KH * D, KH * D)], kvb.at[0, 0, rows(u), :], loc_sem.at[2]
-        ),
-        pltpu.make_async_copy(
-            v_hbm.at[:, cols(u * KH * D, KH * D)], kvb.at[0, 1, rows(u), :], loc_sem.at[3]
-        ),
-    ]
     own_id = pltpu.make_async_copy(ids_hbm, idb.at[0, u], loc_sem.at[4])
 
     def id_in(k, place, dev):
@@ -145,7 +145,22 @@
             qd_s.at[which, j, k - 1], qd_r.at[which, j, k - 1], dev,
         )
 
+    def h2(j, i, place):
+        return rcopy(
+            kvb.at[0, :, rows(place), cols(j * D, D)], kvb.at[2, :, rows(place), cols(j * D, D)],
+            h2_s.at[j, i], h2_r.at[j, i], at(b + 2, u),
+        )
+
     peers = [(k, lax.rem(u + k, U), lax.rem(u + U - k, U)) for k in range(1, U)]
+    shares = [(0, u)] + [(k, frm) for k, _, frm in peers]
+    for copy in own_kv:
+        copy.wait()
+
+    @pl.when(has_up2)
+    def _():
+        for j in range(KH):
+            h2(j, 0, u).start()
+
     loads[0].wait()
     for k, to, _ in peers:
         id_in(k, u, at(b, to)).start()
@@ -155,7 +170,7 @@
         for k, to, _ in peers:
             for which in range(2):
                 kv_in(k, which, j, u, to, at(b, to)).start()
-    for copy in [own_id] + own_kv + own_q:
+    for copy in [own_id] + own_q:
         copy.start()
 
     for copy in loads[3:]:
@@ -187,11 +202,6 @@
             for k, to, _ in peers:
                 st_in(k, u, to, at(b, to)).start()
 
-    def h2(j):
-        return rcopy(
-            kvb.at[0, :, :, cols(j * D, D)], kvb.at[2, :, :, cols(j * D, D)],
-            h2_s.at[j], h2_r.at[j], at(b + 2, u),
-        )
 
     def h2id():
         return rcopy(idb.at[0], idb.at[2], h2i_s.at[0], h2i_r.at[0], at(b + 2, u))
@@ -217,8 +227,6 @@
     def _():
         ptid().start()
 
-    for copy in own_kv:
-        copy.wait()
     for j in range(KH):
         for k, _, frm in peers:
             for which in range(2):
@@ -226,7 +234,8 @@
 
         @pl.when(has_up2)
         def _():
-            h2(j).start()
+            for k, _, frm in peers:
+                h2(j, k, frm).start()
 
         @pl.when(even)
         def _():
@@ -258,7 +267,8 @@
     def arrive2(j):
         @pl.when(has_down2)
         def _():
-            h2(j).wait_recv()
+            for i, place in shares:
+                h2(j, i, place).wait_recv()
 
             @pl.when(odd == 1)
             def _():
@@ -449,7 +459,8 @@
 
         @pl.when(has_up2)
         def _():
-            h2(j).wait_send()
+            for i, place in shares:
+                h2(j, i, place).wait_send()
 
         @pl.when(sends_mate)
         def _():
@@ -517,7 +528,7 @@
     n = max(U - 1, 1)
     dma = pltpu.SemaphoreType.DMA
     sems = []
-    for shape in [(2, KH, n), (2, KH, n), (n,), (n,), (KH,), (1,), (KH,), (1,), (KH,), (KH,), (KH, n), (2, KH, n)]:
+    for shape in [(2, KH, n), (2, KH, n), (n,), (n,), (KH, U), (1,), (KH,), (1,), (KH,), (KH,), (KH, n), (2, KH, n)]:
         sems += [dma(shape), dma(shape)]
     vm = pltpu.VMEM
     results = pl.pallas_call(

time: 37.9 us -> 37.5 us (0.989)
  Pallas kernels: 37.1 us -> 36.7 us
where the time goes in v4:
time: 37.5 us; the launch traced here: 37.4 us
  Pallas kernels  36.7 us (98%)
  between operations  0.64 us (2%)
    pallas_call x1, Pallas kernels, per_device(): pl.pallas_call(functools.partial(kernel, U, B), out_shape=(jax.ShapeDtype...  34.7 us
    pallas_call x1, Pallas kernels, per_device(): pl.pallas_call(close_kernel, out_shape=tuple((jax.ShapeDtypeStruct(r.shap...  2.01 us

profile of v4, /device:TPU:0, one launch (start us, length us, event | category | flops | bytes accessed | tf_op | source)
XLA Modules:
  0.0 37.4 jit_solution(17696400663080791951)
XLA Ops:
  0.6 34.7 %shard_map.94 = (bf16[128,2048]{1,0:T(8,128)(2,1)}, bf16[128,1024]{1,0:T(8,128)(2,1)}, bf16[128,1024]{1,0:T(8,128)(2,1)}) custom-call(bf16[128,2048]{1,0:T(8,128)(2,1)} %q_ref.1, bf16[128,2048]{1,0:T(8,128)(2,1)} %do_hbm.1, bf16[128,1024]{1,0:T(8,128)(2,1)} %k_hbm.1, bf16[128,1024]{1,0:T(8,128)(2,1)} %v_hbm.1, bf16[128,2048]{1,0:T(8,128)(2,1)} %out_hbm.1, ...), custom_call_target="tpu_custom_call" | custom-call | tf_op jit(solution)/shard_map/pallas_call | solution.py:534
  35.4 2.0 %shard_map.95 = (bf16[128,2048]{1,0:T(8,128)(2,1)}, bf16[128,1024]{1,0:T(8,128)(2,1)}, bf16[128,1024]{1,0:T(8,128)(2,1)}) custom-call(bf16[128,2048]{1,0:T(8,128)(2,1)} %get-tuple-element.6.a_in, bf16[128,1024]{1,0:T(8,128)(2,1)} %get-tuple-element.7.b_in, bf16[128,1024]{1,0:T(8,128)(2,1)} %get-tuple-element.8.c_in), custom_call_target="tpu_custom_call" | custom-call | tf_op jit(solution)/shard_map/pallas_call | solution.py:574
